TPU v7x, 32 devices: a whole 2x2x4 slice. The times are simulated.
32 devices in a mesh: segment: 4 (over y, core), shard: 8 (over z, x).
Axes of the slice: x: 2, y: 2, z: 4, core: 2. Of those that a mesh axis runs over, the one named last changes fastest.
Arguments:
- buffer: bfloat16 [8, 18432, 2304], P('segment', 'shard'), may hold values from -6 to 6
- right_basis: bfloat16 [8, 2304, 256], P('segment', 'shard'), may hold values from -0.125 to 0.125
- layer_count: int32 [4], P('segment'), may hold values from 1 to 2, as said below
Outputs:
- momentum_out: bfloat16 [8, 18432, 2304], P('segment', 'shard')
- left_step: bfloat16 [8, 18432, 256], P('segment', 'shard')
- right_step: float32 [8, 2304, 256], P('segment', 'shard')
Inputs may be any that keep to these rules, and one draw needn't show every extreme that they name: `layer_count`: each segment uses between 1 and 2 slots; some segment uses 2 and some segment uses 1.
All inputs are finite; a program needn't handle non-finite values.
Results may differ from a plain program's by a relative error of at most 0.0024.
Values may be sent and summed in bfloat16 or wider, within the bound.
A program may use at most 128 MiB of HBM per device.

v0:
```python
import math

import jax
import jax.numpy as jnp
from jax import lax
from jax.sharding import PartitionSpec as P

MOMENTUM = 0.9
CLIP_RMS = 0.35
SQUARE_FLOOR = 0.0625


def finish_basis(proj, gram):
    lower = jnp.linalg.cholesky(gram)
    solved = jax.scipy.linalg.solve_triangular(lower, jnp.swapaxes(proj, 1, 2), lower=True)
    return jnp.swapaxes(solved, 1, 2)


def right_factor(partial_value):
    groups = lax.axis_size("shard")
    cols = partial_value.shape[1]
    width = cols // groups
    full = lax.psum(partial_value, "shard")
    colsq = jnp.sum(full * full, axis=1, keepdims=True)
    scaled = full * (math.sqrt(cols) * lax.rsqrt(colsq + 1.0))
    local = lax.dynamic_slice_in_dim(scaled, lax.axis_index("shard") * width, width, 1)
    return (full.astype(jnp.bfloat16), local)


def finish_layers(block, proj, gram, used, clip, rows_all):
    ortho = finish_basis(proj, gram)
    half_left = ortho.astype(jnp.bfloat16)
    partial_value = jnp.einsum("kij,kir->kjr", block, half_left, preferred_element_type=jnp.float32)
    half_right, right_local = right_factor(partial_value)
    correction = jnp.einsum(
        "kir,kjr->kij", half_left, half_right, preferred_element_type=jnp.float32
    )
    keep = used[:, None, None]
    moment = jnp.where(keep, block - (1.0 - MOMENTUM) * correction, 0.0).astype(jnp.bfloat16)
    left = jnp.where(keep, clip * math.sqrt(rows_all) * ortho, 0.0).astype(jnp.bfloat16)
    right = jnp.where(keep, right_local, 0.0)
    return (moment, left, right)


def body(buffer, right_basis, layer_count):
    slots = buffer.shape[0]
    rows_dev = buffer.shape[1]
    cols = buffer.shape[2]
    rows_all = rows_dev * lax.axis_size("shard")
    count = layer_count[0]
    used = jnp.arange(slots, dtype=jnp.int32) < count
    per_slot = jnp.sum(jnp.square(buffer.astype(jnp.float32)), axis=(1, 2))
    local_sq = jnp.sum(jnp.where(used, per_slot, 0.0))
    local_elems = count.astype(jnp.float32) * float(rows_dev * cols)
    total_sq, total_elems = lax.psum((local_sq, local_elems), ("segment", "shard"))
    clip = jnp.minimum(1.0, CLIP_RMS * lax.rsqrt(jnp.maximum(total_sq / total_elems, SQUARE_FLOOR)))
    proj = jnp.einsum(
        "kij,kjr->kir",
        buffer,
        lax.all_gather(right_basis, "shard", axis=1, tiled=True),
        preferred_element_type=jnp.float32,
    )
    local_gram = jnp.einsum("kir,kis->krs", proj, proj, precision=lax.Precision.HIGHEST)
    gram = lax.psum(local_gram, "shard")
    return finish_layers(buffer, proj, gram, used, clip, rows_all)


def solution(mesh):
    in_specs = (P("segment", "shard", None), P("segment", "shard", None), P("segment"))
    out_specs = (
        P("segment", "shard", None),
        P("segment", "shard", None),
        P("segment", "shard", None),
    )
    return jax.shard_map(body, mesh=mesh, in_specs=in_specs, out_specs=out_specs, check_vma=False)
```

profile of v0, /device:TPU:0, one launch (start us, length us, event | category | flops | bytes accessed | tf_op | source)
XLA Modules:
  0.0 498.3 jit_solution(15562166234760625701)
XLA Ops:
  7.2 0.0 all-gather.2.cloned.1.call-start
  7.2 0.7 all-gather.2.cloned.1.call-update
  7.9 0.0 all-reduce.5.cloned.1.call-start
  7.9 56.8 %all-gather.2.cloned.1.call-done = bf16[2,2304,256]{2,1,0:T(8,128)(2,1)} async-done(((bf16[2,288,256]{2,1,0:T(8,128)(2,1)}), bf16[2,2304,256]{2,1,0:T(8,128)(2,1)}) %all-gather.2.cloned.1.call-update) | async-done | bytes 2359312 | tf_op jit(solution)/shard_map/all_gather | solution.py:60
  64.7 10.6 %fusion.20 = f32[2,2304,256]{2,1,0:T(8,128)S(1)} fusion(bf16[2,2304,2304]{2,1,0:T(8,128)(2,1)} %param.3, bf16[2,2304,256]{2,1,0:T(8,128)(2,1)} %all-gather.2.cloned.1.call-done), kind=kOutput, calls=%fused_computation.47 | convolution fusion | flops 5435817984 | bytes 28311552 | tf_op jit(solution)/shard_map/kij,kjr->kir/dot_general | solution.py:57
  75.4 0.0 copy-start
  75.4 2.2 copy-done
  77.6 8.4 %fusion.21 = f32[2,256,256]{1,2,0:T(8,128)} fusion(f32[2,2304,256]{2,1,0:T(8,128)S(1)} %fusion.20), kind=kOutput, calls=%fused_computation.48 | convolution fusion | flops 3623878656 | bytes 5242880 | tf_op jit(solution)/shard_map/kir,kis->krs/dot_general | solution.py:63
  86.0 0.0 all-reduce.5.cloned.1.call-update
  86.0 0.2 all-reduce.7.cloned.1.call-start
  86.3 71.0 %all-reduce.5.cloned.1.call-done = f32[2,256,256]{1,2,0:T(8,128)} async-done(((f32[2,256,256]{1,2,0:T(8,128)}), f32[2,256,256]{1,2,0:T(8,128)}) %all-reduce.5.cloned.1.call-update) | async-done | bytes 524304 | tf_op jit(solution)/shard_map/psum | solution.py:64
  157.3 1.2 copy.22
  158.6 1.1 fusion.9
  159.7 23.5 %custom-call.17 = f32[2,128,128]{2,1,0:T(8,128)S(1)} custom-call(f32[2,128,128]{2,1,0:T(8,128)S(1)} %cholesky.122), custom_call_target="Cholesky" | custom-call | tf_op jit(solution)/shard_map/jit(cholesky)/cholesky | solution.py:14
  183.2 19.7 %custom-call.18 = f32[2,1,128,128]{2,3,1,0:T(8,128)S(1)} custom-call(f32[2,1,128,128]{3,2,1,0:T(8,128)S(1)} %select_bitcast_fusion), custom_call_target="InvertDiagBlocksLowerTriangular" | custom-call | tf_op jit(solution)/shard_map/jit(cholesky)/cholesky | solution.py:14
  202.9 0.3 constant_dynamic-update-slice_fusion.1
  203.2 0.4 convolution_subtract_fusion.1
  203.6 23.5 %custom-call.19 = f32[2,128,128]{2,1,0:T(8,128)S(1)} custom-call(f32[2,128,128]{2,1,0:T(8,128)S(1)} %convolution_subtract_fusion.1), custom_call_target="Cholesky" | custom-call | tf_op jit(solution)/shard_map/jit(cholesky)/cholesky | solution.py:14
  227.1 0.2 compare_reduce_fusion
  227.3 0.1 select_select_fusion
  227.4 0.1 triangular_solve.62
  227.5 4.1 while.1
  227.5 0.6 fusion.32
  228.1 1.4 bitcast_dynamic-update-slice_fusion.2
  229.6 0.6 fusion.32
  230.2 1.4 bitcast_dynamic-update-slice_fusion.2
  231.6 39.5 %custom-call.20 = f32[2,2,128,128]{2,3,1,0:T(8,128)S(1)} custom-call(f32[2,2,128,128]{3,2,1,0:T(8,128)S(1)} %bitcast.52), custom_call_target="InvertDiagBlocksLowerTriangular" | custom-call | tf_op jit(solution)/shard_map/jit(_solve_triangular)/vmap()/triangular_solve | solution.py:15
  271.2 0.0 copy-start.1
  271.2 4.0 fusion.5
  275.1 0.0 copy-done.1
  275.2 3.9 convolution_subtract_fusion
  279.1 2.2 fusion.13
  281.3 0.0 copy-start.2
  281.3 1.4 copy-done.2
  282.8 12.2 %convolution_bitcast_fusion = f32[2,2304,256]{1,2,0:T(8,128)} fusion(bf16[2,2304,2304]{2,1,0:T(8,128)(2,1)} %param.3, f32[2,128,2304]{2,1,0:T(8,128)S(1)} %fusion.13, f32[2,128,2304]{2,1,0:T(8,128)S(1)} %fusion.5), kind=kOutput, calls=%fused_computation.7 | convolution fusion | flops 5440536576 | bytes 30670848 | tf_op jit(solution)/shard_map/kij,kir->kjr/dot_general | solution.py:33
  295.0 0.0 all-reduce.7.cloned.1.call-update
  295.7 13.7 %fusion.2 = f32[2]{0:T(128)S(1)} fusion(bf16[2,2304,2304]{2,1,0:T(8,128)(2,1)} %param.3), kind=kLoop, calls=%fused_computation.6 | loop fusion | flops 31850494 | bytes 21233672 | tf_op jit(solution)/shard_map/reduce_sum | solution.py:52
  309.4 0.6 select_reduce_fusion.2
  310.0 43.3 %all-reduce.1 = (f32[]{:T(128)}, f32[]{:T(128)}) all-reduce(f32[]{:T(128)} %select_reduce_fusion.2, f32[]{:T(128)S(6)} %mul.46), channel_id=1, replica_groups=mesh['segment'=4,'shard'=8] {'segment','shard'}, use_global_device_ids=true, to_apply=%region_8.9 | all-reduce | flops 2 | bytes 16 | tf_op jit(solution)/shard_map/psum | solution.py:55
  354.6 3.6 fusion.4
  358.2 4.3 copy.32
  362.6 102.3 %all-reduce.7.cloned.1.call-done = f32[2,2304,256]{1,2,0:T(8,128)} async-done(((f32[2,2304,256]{1,2,0:T(8,128)}), f32[2,2304,256]{1,2,0:T(8,128)}) %all-reduce.7.cloned.1.call-update) | async-done | bytes 4718608 | tf_op jit(solution)/shard_map/psum | solution.py:23
  464.8 2.7 multiply_reduce_fusion
  467.5 1.6 fusion.8
  469.1 1.1 copy.33
  470.2 21.2 %fusion.1 = bf16[2,2304,2304]{2,1,0:T(8,128)(2,1)} fusion(bf16[2,2304,2304]{2,1,0:T(8,128)(2,1)} %param.3, pred[2]{0:T(512)(128)(4,1)S(1)} %iota_compare_fusion.3, f32[2,2304,256]{1,2,0:T(8,128)} %all-reduce.7.cloned.1.call-done, f32[2,128,2304]{2,1,0:T(8,128)} %copy-done.2, f32[2,128,2304]{2,1,0:T(8,128)S(1)} %fusion.5), kind=kOutput, calls=%fused_computation.5 | convolution fusion | flops 5494800384 | bytes 51904512 | tf_op jit(solution)/shard_map/kir,kjr->kij/dot_general | solution.py:35
  (14 shorter events, 0.2 us)
Async XLA Ops:
  7.2 57.6 %all-gather.2.cloned.1.call-start = ((), (), s32[]{:S(2)}) async-start(), calls=%async_computation | async-start | bytes 2654208 | tf_op jit(solution)/shard_map/all_gather | solution.py:60
  7.9 149.4 %all-reduce.5.cloned.1.call-start = ((), (), s32[]{:S(2)}) async-start(), calls=%async_computation.1 | async-start | bytes 1048576 | tf_op jit(solution)/shard_map/psum | solution.py:64
  75.4 2.2 copy-start
  86.0 378.8 %all-reduce.7.cloned.1.call-start = ((), (), s32[]{:S(2)}) async-start(), calls=%async_computation.2 | async-start | bytes 9437184 | tf_op jit(solution)/shard_map/psum | solution.py:23
  271.2 4.0 copy-start.1
  281.3 1.4 copy-start.2
Sparse Core Ops, SparseCore 0:
  10.2 54.5 all-gather.1
  86.1 71.1 all-reduce.4
  295.1 169.6 all-reduce.6
where the time goes:
time: 506 us; the launch traced here: 498 us
  waiting for transfers between devices  231 us (46%)
  other arithmetic  130 us (26%)
  matrix products  63.2 us (12%)
  blocking collectives  43.3 us (9%)
  between operations  16.4 us (3%)
  local copies, waits for them, and re-layouts  14.4 us (3%)
    psum x1, waiting for transfers between devices, right_factor(): full = lax.psum(partial_value, 'shard')  102 us
    psum x1, waiting for transfers between devices, body(): gram = lax.psum(local_gram, 'shard')  71 us
    another operation x9, other arithmetic, finish_basis(): lower = jnp.linalg.cholesky(gram)  66.8 us
    all_gather x1, waiting for transfers between devices, body(): lax.all_gather(right_basis, 'shard', axis=1, tiled=True)  56.8 us
    psum x1, blocking collectives, body(): lax.psum((local_sq, local_elems), ('segment', 'shard'))  43.3 us
    another operation x4, other arithmetic, finish_basis(): jax.scipy.linalg.solve_triangular(lower, jnp.swapaxes(proj, 1, 2), lower=...  39.7 us
    dot_general x1, matrix products, finish_layers(): jnp.einsum('kir,kjr->kij', half_left, half_right, preferred_element_type=...  21.2 us
    reduce_sum x1, other arithmetic, body(): per_slot = jnp.sum(jnp.square(buffer.astype(jnp.float32)), axis=(1, 2))  13.7 us
  transfers between devices with their start and end apart: 3, of which 3 were waited for; matrix products, arithmetic and copies ran while one was open for 4% of the time, Pallas kernels for 0%

commit v1 on v0

v1 whole, which is shorter than its diff:
```python
import functools
import math

import jax
import jax.numpy as jnp
from jax import lax
from jax.experimental import pallas as pl
from jax.experimental.pallas import tpu as pltpu
from jax.sharding import PartitionSpec as P

MOMENTUM = 0.9
CLIP_RMS = 0.35
SQUARE_FLOOR = 0.0625
MESH = pl.DeviceIdType.MESH
HIGHEST = lax.Precision.HIGHEST
F32 = jnp.float32
BF16 = jnp.bfloat16
LINK = jnp.float32
VMEM_LIMIT = 60 * 1024 * 1024


def to_index(pos, n):
    if n % 2:
        return pos
    return jnp.where(pos < n // 2, 2 * pos, 2 * (n - 1 - pos) + 1)


def to_pos(index, n):
    if n % 2:
        return index
    return jnp.where(index % 2 == 0, index // 2, n - 1 - index // 2)


def hops_of(slot, way, n):
    return n // 2 if slot % 2 == way else n - 1 - n // 2


def greet(devices):
    barrier = pltpu.get_barrier_semaphore()
    for axis, index in devices:
        pl.semaphore_signal(barrier, inc=1, device_id={axis: index}, device_id_type=MESH)
    pl.semaphore_wait(barrier, len(devices))


def ring(n):
    me = lax.axis_index("shard")
    pos = to_pos(me, n)
    right = to_index((pos + 1) % n, n)
    left = to_index((pos + n - 1) % n, n)
    return me, pos, (right, left)


def ring_gather(n, slots, out_ref, send, recv):
    me, pos, sides = ring(n)
    started = {}
    for hop in range(n // 2 + 1):
        for slot in range(slots):
            for way in range(2):
                total = hops_of(slot, way, n)
                if hop > total:
                    continue
                if hop > 0:
                    started[slot, way, hop - 1].wait_recv()
                if hop == total:
                    continue
                sign = -1 if way == 0 else 1
                owner = to_index((pos + sign * hop + n) % n, n)
                block = out_ref.at[slot, owner]
                copy = pltpu.make_async_remote_copy(
                    src_ref=block,
                    dst_ref=block,
                    send_sem=send.at[slot, way, hop],
                    recv_sem=recv.at[slot, way, hop],
                    device_id={"shard": sides[way]},
                    device_id_type=MESH,
                )
                copy.start()
                started[slot, way, hop] = copy
    for copy in started.values():
        copy.wait_send()


def ring_scatter(n, slots, part_ref, sums, got, send, recv):
    me, pos, sides = ring(n)
    started = {}
    for hop in range(n // 2):
        for slot in range(slots):
            for way in range(2):
                total = hops_of(slot, way, n)
                if hop >= total:
                    continue
                sign = 1 if way == 0 else -1
                owner = to_index((pos + sign * (total - hop) + n) % n, n)
                value = part_ref[slot, owner]
                if hop > 0:
                    started[slot, way, hop - 1].wait_recv()
                    value = value + got[slot, way, hop - 1].astype(F32)
                sums[slot, way, hop] = value.astype(sums.dtype)
                copy = pltpu.make_async_remote_copy(
                    src_ref=sums.at[slot, way, hop],
                    dst_ref=got.at[slot, way, hop],
                    send_sem=send.at[slot, way, hop],
                    recv_sem=recv.at[slot, way, hop],
                    device_id={"shard": sides[way]},
                    device_id_type=MESH,
                )
                copy.start()
                started[slot, way, hop] = copy
    out = []
    for slot in range(slots):
        value = part_ref[slot, me]
        for way in range(2):
            last = hops_of(slot, way, n) - 1
            if last >= 0:
                started[slot, way, last].wait_recv()
                value = value + got[slot, way, last].astype(F32)
        out.append(value)
    for copy in started.values():
        copy.wait_send()
    return out


def exchange(axis, n, source, landing, send, recv):
    me = lax.axis_index(axis)
    copies = []
    for step in range(1, n):
        peer = (me + step) % n
        copy = pltpu.make_async_remote_copy(
            src_ref=source(peer),
            dst_ref=landing.at[me],
            send_sem=send.at[step],
            recv_sem=recv.at[step],
            device_id={axis: peer},
            device_id_type=MESH,
        )
        copy.start()
        copies.append(copy)
    return copies


def others(axis, n):
    me = lax.axis_index(axis)
    return [(axis, (me + step) % n) for step in range(1, n)]


def gather_kernel(n, slots, basis_ref, out_ref, send, recv, local):
    me, _, sides = ring(n)
    copy = pltpu.make_async_copy(basis_ref, out_ref.at[:, me], local)
    copy.start()
    greet([("shard", sides[0]), ("shard", sides[1])])
    copy.wait()
    ring_gather(n, slots, out_ref, send, recv)


def project_kernel(block_ref, basis_ref, proj_ref, gram_ref, part_ref, square_ref):
    block = block_ref[0]
    proj = jnp.dot(block, basis_ref[0], preferred_element_type=F32)
    proj_ref[0] = proj
    gram = lax.dot_general(
        proj, proj, (((0,), (0,)), ((), ())), precision=HIGHEST, preferred_element_type=F32
    )
    part = lax.dot_general(
        block, proj.astype(BF16), (((0,), (0,)), ((), ())), preferred_element_type=F32
    )
    wide = block.astype(F32)
    square = jnp.sum(jnp.square(wide).reshape(-1, 8, wide.shape[1]), axis=0)

    @pl.when(pl.program_id(1) == 0)
    def _():
        gram_ref[0] = gram
        part_ref[0] = part
        square_ref[0] = square

    @pl.when(pl.program_id(1) > 0)
    def _():
        gram_ref[0] += gram
        part_ref[0] += part
        square_ref[0] += square


def reduce_kernel(
    n, segments, slots, gram_ref, stat_ref, part_ref, full_ref, total_ref, own_ref,
    landing, done, stat_in, stat_sum, seg_in, sums, got,
    send_a, recv_a, send_b, recv_b, send_c, recv_c, send_d, recv_d, send_e, recv_e,
):
    me = lax.axis_index("shard")
    seg = lax.axis_index("segment")
    greet(others("shard", n) + others("segment", segments))
    first = exchange("shard", n, lambda peer: gram_ref.at[peer], landing, send_a, recv_a)
    stats = exchange("shard", n, lambda peer: stat_ref, stat_in, send_b, recv_b)
    landing[me] = gram_ref[me]
    stat_in[me] = stat_ref[...]
    for copy in first:
        copy.wait()
    value = landing[0]
    for i in range(1, n):
        value = value + landing[i]
    done[...] = value
    full_ref[me] = value
    second = exchange("shard", n, lambda peer: done, full_ref, send_c, recv_c)
    for copy in stats:
        copy.wait()
    value = stat_in[0]
    for i in range(1, n):
        value = value + stat_in[i]
    stat_sum[...] = value
    seg_in[seg] = value
    last = exchange("segment", segments, lambda peer: stat_sum, seg_in, send_d, recv_d)
    own = ring_scatter(n, slots, part_ref, sums, got, send_e, recv_e)
    for slot in range(slots):
        own_ref[slot] = own[slot]
    for copy in last + second:
        copy.wait()
    value = seg_in[0]
    for i in range(1, segments):
        value = value + seg_in[i]
    total_ref[...] = value


def eliminate(blocks):
    size = blocks[0].shape[0]
    rows = lax.broadcasted_iota(jnp.int32, (size, size), 0)
    lanes = lax.broadcasted_iota(jnp.int32, (size, size), 1)

    def step(j, blocks):
        out = []
        for m in blocks:
            row = jnp.sum(jnp.where(rows == j, m, 0.0), axis=0, keepdims=True)
            col = jnp.sum(jnp.where(lanes == j, m, 0.0), axis=1, keepdims=True)
            lane = lanes[:1] == j
            pivot = jnp.sum(jnp.where(lane, row, 0.0), axis=1, keepdims=True)
            scaled = jnp.where(lane, 1.0, row) / pivot
            below = rows > j
            kept = jnp.where(below & (lanes == j), 0.0, m)
            out.append(kept - jnp.where(below, col, 0.0) * scaled)
        return tuple(out)

    blocks = lax.fori_loop(0, size, step, tuple(blocks))
    result = []
    for m in blocks:
        diag = jnp.sum(jnp.where(lanes == rows, m, 0.0), axis=1, keepdims=True)
        unit = jnp.where(lanes < rows, m, jnp.where(lanes == rows, 1.0, 0.0))
        result.append(unit * lax.rsqrt(diag))
    return result


def mm(a, b, dims):
    return lax.dot_general(a, b, ((dims[:1], dims[1:]), ((), ())), precision=HIGHEST, preferred_element_type=F32)


def factor_kernel(slots, gram_ref, inv_ref):
    half = gram_ref.shape[1] // 2
    heads = eliminate([gram_ref[s, :half, :half] for s in range(slots)])
    sides = [mm(gram_ref[s, half:, :half], heads[s], (1, 1)) for s in range(slots)]
    rests = [gram_ref[s, half:, half:] - mm(sides[s], sides[s], (1, 1)) for s in range(slots)]
    tails = eliminate(rests)
    for s in range(slots):
        inv_ref[s, :half, :half] = heads[s]
        inv_ref[s, :half, half:] = jnp.zeros((half, half), F32)
        inv_ref[s, half:, :half] = -mm(tails[s], mm(sides[s], heads[s], (1, 0)), (1, 0))
        inv_ref[s, half:, half:] = tails[s]


def right_kernel(
    n, slots, cols, own_ref, inv_ref, right_ref, full_ref, mine, sq_in, send_a, recv_a, send_b, recv_b
):
    me, _, sides = ring(n)
    greet(others("shard", n))
    values = []
    mine[...] = jnp.zeros_like(mine)
    for slot in range(slots):
        value = mm(own_ref[slot], inv_ref[slot], (1, 1))
        full_ref[slot, me] = value.astype(BF16)
        mine[slot : slot + 1] = jnp.sum(value * value, axis=0, keepdims=True)
        right_ref[slot] = value
    copies = exchange("shard", n, lambda peer: mine, sq_in, send_a, recv_a)
    sq_in[me] = mine[...]
    ring_gather(n, slots, full_ref, send_b, recv_b)
    for copy in copies:
        copy.wait()
    total = sq_in[0]
    for i in range(1, n):
        total = total + sq_in[i]
    scale = math.sqrt(cols) * lax.rsqrt(total + 1.0)
    for slot in range(slots):
        right_ref[slot] = right_ref[slot] * scale[slot : slot + 1]


def final_kernel(scale_ref, count_ref, block_ref, proj_ref, inv_ref, basis_ref, moment_ref, left_ref):
    keep = pl.program_id(0) < count_ref[0]

    @pl.when(keep)
    def _():
        ortho = mm(proj_ref[0], inv_ref[0], (1, 1))
        half = ortho.astype(BF16)
        fix = lax.dot_general(half, basis_ref[0], (((1,), (1,)), ((), ())), preferred_element_type=F32)
        moment_ref[0] = (block_ref[0].astype(F32) - (1.0 - MOMENTUM) * fix).astype(BF16)
        left_ref[0] = (scale_ref[0] * ortho).astype(BF16)

    @pl.when(jnp.logical_not(keep))
    def _():
        moment_ref[...] = jnp.zeros_like(moment_ref)
        left_ref[...] = jnp.zeros_like(left_ref)


def vmem():
    return pl.BlockSpec(memory_space=pltpu.VMEM)


def comm(collective_id):
    return pltpu.CompilerParams(
        collective_id=collective_id, has_side_effects=True, vmem_limit_bytes=VMEM_LIMIT
    )


def body(buffer, right_basis, layer_count):
    n = lax.axis_size("shard")
    segments = lax.axis_size("segment")
    slots, rows_dev, cols = buffer.shape
    width, rank = right_basis.shape[1:]
    rows_all = rows_dev * n
    dma = pltpu.SemaphoreType.DMA
    hops = max(n // 2, 1)
    shape = jax.ShapeDtypeStruct
    count = layer_count[0]

    basis = pl.pallas_call(
        functools.partial(gather_kernel, n, slots),
        out_shape=shape((slots, n, width, rank), BF16),
        in_specs=[vmem()],
        out_specs=vmem(),
        scratch_shapes=[dma((slots, 2, hops)), dma((slots, 2, hops)), dma],
        compiler_params=comm(0),
        name="gather_basis",
    )(right_basis).reshape(slots, cols, rank)

    tile = math.gcd(rows_dev, 256)
    tiles = rows_dev // tile
    per_tile = pl.BlockSpec((1, tile, cols), lambda s, i: (s, i, 0))
    proj_tile = pl.BlockSpec((1, tile, rank), lambda s, i: (s, i, 0))

    def per_slot(*dims):
        return pl.BlockSpec((1,) + dims, lambda s, i: (s, 0, 0))

    proj, gram, part, square = pl.pallas_call(
        project_kernel,
        grid=(slots, tiles),
        out_shape=(
            shape((slots, rows_dev, rank), F32),
            shape((slots, rank, rank), F32),
            shape((slots, cols, rank), F32),
            shape((slots, 8, cols), F32),
        ),
        in_specs=[per_tile, per_slot(cols, rank)],
        out_specs=(proj_tile, per_slot(rank, rank), per_slot(cols, rank), per_slot(8, cols)),
        compiler_params=pltpu.CompilerParams(vmem_limit_bytes=VMEM_LIMIT),
        name="project",
    )(buffer, basis)

    used = jnp.arange(slots, dtype=jnp.int32) < count
    local_sq = jnp.sum(jnp.where(used, jnp.sum(square, axis=(1, 2)), 0.0))
    local_elems = count.astype(F32) * float(rows_dev * cols)
    odd = lax.broadcasted_iota(jnp.int32, (8, 128), 0) % 2 == 1
    stat = jnp.where(odd, local_elems, local_sq)
    chunk = slots * rank // n

    full_gram, total, own = pl.pallas_call(
        functools.partial(reduce_kernel, n, segments, slots),
        out_shape=(
            shape((n, chunk, rank), F32),
            shape((8, 128), F32),
            shape((slots, width, rank), F32),
        ),
        in_specs=[vmem()] * 3,
        out_specs=(vmem(),) * 3,
        scratch_shapes=[
            pltpu.VMEM((n, chunk, rank), F32),
            pltpu.VMEM((chunk, rank), F32),
            pltpu.VMEM((n, 8, 128), F32),
            pltpu.VMEM((8, 128), F32),
            pltpu.VMEM((segments, 8, 128), F32),
            pltpu.VMEM((slots, 2, hops, width, rank), LINK),
            pltpu.VMEM((slots, 2, hops, width, rank), LINK),
            dma((n,)), dma((n,)), dma((n,)), dma((n,)), dma((n,)), dma((n,)),
            dma((segments,)), dma((segments,)),
            dma((slots, 2, hops)), dma((slots, 2, hops)),
        ],
        compiler_params=comm(1),
        name="reduce",
    )(gram.reshape(n, chunk, rank), stat, part.reshape(slots, n, width, rank))

    inverse = pl.pallas_call(
        functools.partial(factor_kernel, slots),
        out_shape=shape((slots, rank, rank), F32),
        in_specs=[vmem()],
        out_specs=vmem(),
        name="factor",
    )(full_gram.reshape(slots, rank, rank))

    right, half_right = pl.pallas_call(
        functools.partial(right_kernel, n, slots, cols),
        out_shape=(shape((slots, width, rank), F32), shape((slots, n, width, rank), BF16)),
        in_specs=[vmem()] * 2,
        out_specs=(vmem(),) * 2,
        scratch_shapes=[
            pltpu.VMEM((8, rank), F32),
            pltpu.VMEM((n, 8, rank), F32),
            dma((n,)), dma((n,)),
            dma((slots, 2, hops)), dma((slots, 2, hops)),
        ],
        compiler_params=comm(2),
        name="right",
    )(own, inverse)

    clip = jnp.minimum(1.0, CLIP_RMS * lax.rsqrt(jnp.maximum(total[0, 0] / total[1, 0], SQUARE_FLOOR)))
    scale = (clip * math.sqrt(rows_all)).reshape(1)
    smem = pl.BlockSpec(memory_space=pltpu.SMEM)
    moment, left = pl.pallas_call(
        final_kernel,
        grid=(slots, tiles),
        out_shape=(shape(buffer.shape, BF16), shape((slots, rows_dev, rank), BF16)),
        in_specs=[smem, smem, per_tile, proj_tile, per_slot(rank, rank), per_slot(cols, rank)],
        out_specs=(per_tile, proj_tile),
        compiler_params=pltpu.CompilerParams(vmem_limit_bytes=VMEM_LIMIT),
        name="final",
    )(scale, layer_count, buffer, proj, inverse, half_right.reshape(slots, cols, rank))
    return (moment, left, jnp.where(used[:, None, None], right, 0.0))


def solution(mesh):
    in_specs = (P("segment", "shard", None), P("segment", "shard", None), P("segment"))
    out_specs = (
        P("segment", "shard", None),
        P("segment", "shard", None),
        P("segment", "shard", None),
    )
    return jax.shard_map(body, mesh=mesh, in_specs=in_specs, out_specs=out_specs, check_vma=False)
```

time: 506 us -> 261 us (0.52)
  Pallas kernels: 0 us -> 249 us
  waiting for transfers between devices: 231 us -> 0 us
  other arithmetic: 130 us -> 4.99 us
  matrix products: 63.2 us -> 0 us
  blocking collectives: 43.3 us -> 0 us
  between operations: 16.4 us -> 2.71 us
  local copies, waits for them, and re-layouts: 14.4 us -> 1.27 us
    pallas_call x0 -> x6, Pallas kernels: none -> 249 us  [the longest x1 77.9 us: body(): pl.pallas_call(functools.partial(reduce_kernel, n, segments, slots), out_...]
    psum x2 -> x0, waiting for transfers between devices: 173 us -> none  [the longest x1 102 us: right_factor(): full = lax.psum(partial_value, 'shard')]
    another operation x13 -> x0, other arithmetic: 107 us -> none  [the longest x9 66.8 us: finish_basis(): lower = jnp.linalg.cholesky(gram)]
    all_gather x1 -> x0, waiting for transfers between devices: 56.8 us -> none  [body(): lax.all_gather(right_basis, 'shard', axis=1, tiled=True)]
    dot_general x4 -> x0, matrix products: 52.4 us -> none  [the longest x1 21.2 us: finish_layers(): jnp.einsum('kir,kjr->kij', half_left, half_right, preferred_element_type=...]
    psum x1 -> x0, blocking collectives: 43.3 us -> none  [body(): lax.psum((local_sq, local_elems), ('segment', 'shard'))]
    reduce_sum x3 -> x2, other arithmetic: 17.1 us -> 1.69 us  [body(): local_sq = jnp.sum(jnp.where(used, jnp.sum(square, axis=(1, 2)), 0.0))]
    another operation x5 -> x0, matrix products: 10.8 us -> none  [the longest x3 10.1 us: finish_basis(): jax.scipy.linalg.solve_triangular(lower, jnp.swapaxes(proj, 1, 2), lower=...]
  transfers between devices with their start and end apart: 3 -> 0, of which waited for: 3 -> 0; matrix products, arithmetic and copies ran while one was open for 4% -> 0% of each run, Pallas kernels for 0% -> 0%
where the time goes in v1:
time: 261 us; the launch traced here: 258 us
  Pallas kernels  249 us (95%)
  other arithmetic  4.99 us (2%)
  between operations  2.71 us (1%)
    pallas_call x1, Pallas kernels, body(): pl.pallas_call(functools.partial(reduce_kernel, n, segments, slots), out_...  77.9 us
    pallas_call x1, Pallas kernels, body(): pl.pallas_call(project_kernel, grid=(slots, tiles), out_shape=(shape((slo...  40 us
    pallas_call x1, Pallas kernels, body(): pl.pallas_call(functools.partial(factor_kernel, slots), out_shape=shape((...  37.2 us
    pallas_call x1, Pallas kernels, body(): pl.pallas_call(functools.partial(right_kernel, n, slots, cols), out_shape...  36.3 us
    pallas_call x1, Pallas kernels, body(): pl.pallas_call(functools.partial(gather_kernel, n, slots), out_shape=shap...  31.5 us
    pallas_call x1, Pallas kernels, body(): pl.pallas_call(final_kernel, grid=(slots, tiles), out_shape=(shape(buffer...  26.5 us

profile of v1, /device:TPU:0, one launch (start us, length us, event | category | flops | bytes accessed | tf_op | source)
XLA Modules:
  0.0 258.3 jit_solution(8579813219389405364)
XLA Ops:
  1.3 31.5 %gather_basis.1 = bf16[2,8,288,256]{3,2,1,0:T(8,128)(2,1)} custom-call(bf16[2,288,256]{2,1,0:T(8,128)(2,1)} %basis_ref.1), custom_call_target="tpu_custom_call" | custom-call | tf_op jit(solution)/shard_map/gather_basis/pallas_call | solution.py:327
  32.8 40.0 %project.1 = (f32[2,2304,256]{2,1,0:T(8,128)}, f32[2,256,256]{2,1,0:T(8,128)}, f32[2,2304,256]{2,1,0:T(8,128)}, f32[2,8,2304]{2,1,0:T(8,128)}) custom-call(bf16[2,2304,2304]{2,1,0:T(8,128)(2,1)} %block_ref.3, bf16[2,2304,256]{2,1,0:T(8,128)(2,1)} %bitcast.10), custom_call_target="tpu_custom_call" | custom-call | tf_op jit(solution)/shard_map/project/pallas_call | solution.py:345
  72.8 1.0 reduce_sum.18
  73.8 0.7 select_reduce_fusion
  74.4 1.3 fusion.stat_ref
  75.7 77.9 %reduce.1 = (f32[8,64,256]{2,1,0:T(8,128)}, f32[8,128]{1,0:T(8,128)}, f32[2,288,256]{2,1,0:T(8,128)}) custom-call(f32[8,64,256]{2,1,0:T(8,128)} %bitcast.13, f32[8,128]{1,0:T(8,128)} %fusion.stat_ref, f32[2,8,288,256]{3,2,1,0:T(8,128)} %bitcast.11), custom_call_target="tpu_custom_call" | custom-call | tf_op jit(solution)/shard_map/reduce/pallas_call | solution.py:367
  153.7 1.3 fusion.1
  156.3 37.2 %factor.1.inv_ref = f32[2,256,256]{2,1,0:T(8,128)} custom-call(f32[2,256,256]{2,1,0:T(8,128)} %bitcast.14), custom_call_target="tpu_custom_call" | custom-call | tf_op jit(solution)/shard_map/factor/pallas_call | solution.py:392
  193.5 36.3 %right.1 = (f32[2,288,256]{2,1,0:T(8,128)}, bf16[2,8,288,256]{3,2,1,0:T(8,128)(2,1)}) custom-call(f32[2,288,256]{2,1,0:T(8,128)} %get-tuple-element.20.own_ref, f32[2,256,256]{2,1,0:T(8,128)} %factor.1.inv_ref), custom_call_target="tpu_custom_call" | custom-call | tf_op jit(solution)/shard_map/right/pallas_call | solution.py:400
  229.8 2.0 broadcast_select_fusion
  231.8 26.5 %final.1 = (bf16[2,2304,2304]{2,1,0:T(8,128)(2,1)}, bf16[2,2304,256]{2,1,0:T(8,128)(2,1)}) custom-call(f32[1]{0:T(128)} %bitcast.4.scale_ref, s32[1]{0:T(128)} %copy.6.count_ref, bf16[2,2304,2304]{2,1,0:T(8,128)(2,1)} %block_ref.3, f32[2,2304,256]{2,1,0:T(8,128)} %get-tuple-element.18.proj_ref, f32[2,256,256]{2,1,0:T(8,128)} %factor.1.inv_ref, ...), custom_call_target="tpu_custom_call" | custom-call | tf_op jit(solution)/shard_map/final/pallas_call | solution.py:418
  (3 shorter events, 0.0 us)

commit v2 on v1

--- a/solution.py
+++ b/solution.py
@@ -80,7 +80,7 @@
         copy.wait_send()
 
 
-def ring_scatter(n, slots, part_ref, sums, got, send, recv):
+def ring_scatter(n, slots, part_ref, sums, got, send, recv, between):
     me, pos, sides = ring(n)
     started = {}
     for hop in range(n // 2):
@@ -106,6 +106,7 @@
                 )
                 copy.start()
                 started[slot, way, hop] = copy
+        between(hop)
     out = []
     for slot in range(slots):
         value = part_ref[slot, me]
@@ -152,72 +153,54 @@
     ring_gather(n, slots, out_ref, send, recv)
 
 
-def project_kernel(block_ref, basis_ref, proj_ref, gram_ref, part_ref, square_ref):
+def split(value):
+    high = value.astype(BF16)
+    return high, (value - high.astype(F32)).astype(BF16)
+
+
+def dot(a, b, dims):
+    return lax.dot_general(a, b, ((dims[:1], dims[1:]), ((), ())), preferred_element_type=F32)
+
+
+def project_kernel(block_ref, basis_ref, proj_ref, gram_ref, part_ref, square_ref, cross):
     block = block_ref[0]
     proj = jnp.dot(block, basis_ref[0], preferred_element_type=F32)
     proj_ref[0] = proj
-    gram = lax.dot_general(
-        proj, proj, (((0,), (0,)), ((), ())), precision=HIGHEST, preferred_element_type=F32
-    )
-    part = lax.dot_general(
-        block, proj.astype(BF16), (((0,), (0,)), ((), ())), preferred_element_type=F32
-    )
+    high, low = split(proj)
+    gram = dot(high, high, (0, 0)) + dot(low, low, (0, 0))
+    mixed = dot(high, low, (0, 0))
+    part = dot(block, high, (0, 0))
     wide = block.astype(F32)
     square = jnp.sum(jnp.square(wide).reshape(-1, 8, wide.shape[1]), axis=0)
+    half = gram.shape[0] // 2
 
     @pl.when(pl.program_id(1) == 0)
     def _():
-        gram_ref[0] = gram
+        cross[0] = gram
+        cross[1] = mixed
         part_ref[0] = part
         square_ref[0] = square
 
     @pl.when(pl.program_id(1) > 0)
     def _():
-        gram_ref[0] += gram
+        cross[0] += gram
+        cross[1] += mixed
         part_ref[0] += part
         square_ref[0] += square
 
-
-def reduce_kernel(
-    n, segments, slots, gram_ref, stat_ref, part_ref, full_ref, total_ref, own_ref,
-    landing, done, stat_in, stat_sum, seg_in, sums, got,
-    send_a, recv_a, send_b, recv_b, send_c, recv_c, send_d, recv_d, send_e, recv_e,
-):
-    me = lax.axis_index("shard")
-    seg = lax.axis_index("segment")
-    greet(others("shard", n) + others("segment", segments))
-    first = exchange("shard", n, lambda peer: gram_ref.at[peer], landing, send_a, recv_a)
-    stats = exchange("shard", n, lambda peer: stat_ref, stat_in, send_b, recv_b)
-    landing[me] = gram_ref[me]
-    stat_in[me] = stat_ref[...]
-    for copy in first:
-        copy.wait()
-    value = landing[0]
-    for i in range(1, n):
-        value = value + landing[i]
-    done[...] = value
-    full_ref[me] = value
-    second = exchange("shard", n, lambda peer: done, full_ref, send_c, recv_c)
-    for copy in stats:
-        copy.wait()
-    value = stat_in[0]
-    for i in range(1, n):
-        value = value + stat_in[i]
-    stat_sum[...] = value
-    seg_in[seg] = value
-    last = exchange("segment", segments, lambda peer: stat_sum, seg_in, send_d, recv_d)
-    own = ring_scatter(n, slots, part_ref, sums, got, send_e, recv_e)
-    for slot in range(slots):
-        own_ref[slot] = own[slot]
-    for copy in last + second:
-        copy.wait()
-    value = seg_in[0]
-    for i in range(1, segments):
-        value = value + seg_in[i]
-    total_ref[...] = value
-
-
-def eliminate(blocks):
+    @pl.when(pl.program_id(1) == pl.num_programs(1) - 1)
+    def _():
+        whole = cross[0] + cross[1] + cross[1].T
+        gram_ref[0, 0] = whole[:half, :half]
+        gram_ref[0, 1] = whole[half:, :half]
+        gram_ref[0, 2] = whole[half:, half:]
+
+
+def mm(a, b, dims):
+    return lax.dot_general(a, b, ((dims[:1], dims[1:]), ((), ())), precision=HIGHEST, preferred_element_type=F32)
+
+
+def eliminate(blocks, first, last):
     size = blocks[0].shape[0]
     rows = lax.broadcasted_iota(jnp.int32, (size, size), 0)
     lanes = lax.broadcasted_iota(jnp.int32, (size, size), 1)
@@ -235,53 +218,112 @@
             out.append(kept - jnp.where(below, col, 0.0) * scaled)
         return tuple(out)
 
-    blocks = lax.fori_loop(0, size, step, tuple(blocks))
-    result = []
-    for m in blocks:
-        diag = jnp.sum(jnp.where(lanes == rows, m, 0.0), axis=1, keepdims=True)
-        unit = jnp.where(lanes < rows, m, jnp.where(lanes == rows, 1.0, 0.0))
-        result.append(unit * lax.rsqrt(diag))
-    return result
-
-
-def mm(a, b, dims):
-    return lax.dot_general(a, b, ((dims[:1], dims[1:]), ((), ())), precision=HIGHEST, preferred_element_type=F32)
-
-
-def factor_kernel(slots, gram_ref, inv_ref):
-    half = gram_ref.shape[1] // 2
-    heads = eliminate([gram_ref[s, :half, :half] for s in range(slots)])
-    sides = [mm(gram_ref[s, half:, :half], heads[s], (1, 1)) for s in range(slots)]
-    rests = [gram_ref[s, half:, half:] - mm(sides[s], sides[s], (1, 1)) for s in range(slots)]
-    tails = eliminate(rests)
-    for s in range(slots):
-        inv_ref[s, :half, :half] = heads[s]
-        inv_ref[s, :half, half:] = jnp.zeros((half, half), F32)
-        inv_ref[s, half:, :half] = -mm(tails[s], mm(sides[s], heads[s], (1, 0)), (1, 0))
-        inv_ref[s, half:, half:] = tails[s]
-
-
-def right_kernel(
-    n, slots, cols, own_ref, inv_ref, right_ref, full_ref, mine, sq_in, send_a, recv_a, send_b, recv_b
+    return lax.fori_loop(first, last, step, tuple(blocks))
+
+
+def inverse_of(m):
+    rows = lax.broadcasted_iota(jnp.int32, m.shape, 0)
+    lanes = lax.broadcasted_iota(jnp.int32, m.shape, 1)
+    diag = jnp.sum(jnp.where(lanes == rows, m, 0.0), axis=1, keepdims=True)
+    unit = jnp.where(lanes < rows, m, jnp.where(lanes == rows, 1.0, 0.0))
+    return unit * lax.rsqrt(diag)
+
+
+def factor_pieces(slots, full_ref, work, side, inv_ref):
+    half = work.shape[1]
+
+    def run(first, last):
+        done = eliminate([work[s] for s in range(slots)], first, last)
+        for s in range(slots):
+            work[s] = done[s]
+
+    def start():
+        grams = full_ref[...].reshape(slots, 3, half, half)
+        for s in range(slots):
+            work[s] = grams[s, 0]
+        run(0, half // 2)
+
+    def turn():
+        run(half // 2, half)
+        grams = full_ref[...].reshape(slots, 3, half, half)
+        for s in range(slots):
+            head = inverse_of(work[s])
+            edge = mm(grams[s, 1], head, (1, 1))
+            inv_ref[s, :half, :half] = head
+            inv_ref[s, :half, half:] = jnp.zeros((half, half), F32)
+            side[s] = mm(edge, head, (1, 0))
+            work[s] = grams[s, 2] - mm(edge, edge, (1, 1))
+
+    def middle():
+        run(0, half // 2)
+
+    def end():
+        run(half // 2, half)
+        for s in range(slots):
+            tail = inverse_of(work[s])
+            inv_ref[s, half:, :half] = -mm(tail, side[s], (1, 0))
+            inv_ref[s, half:, half:] = tail
+
+    return [start, turn, middle, end]
+
+
+def add_up(ref, count):
+    value = ref[0]
+    for i in range(1, count):
+        value = value + ref[i]
+    return value
+
+
+def reduce_kernel(
+    n, segments, slots, cols, gram_ref, stat_ref, part_ref, total_ref, inv_ref, right_ref, basis_ref,
+    full, landing, done, stat_in, stat_sum, seg_in, sums, got, work, side, mine, sq_in,
+    send_a, recv_a, send_b, recv_b, send_c, recv_c, send_d, recv_d, send_e, recv_e,
+    send_f, recv_f, send_g, recv_g,
 ):
-    me, _, sides = ring(n)
-    greet(others("shard", n))
-    values = []
+    me = lax.axis_index("shard")
+    seg = lax.axis_index("segment")
+    greet(others("shard", n) + others("segment", segments))
+    first = exchange("shard", n, lambda peer: gram_ref.at[peer], landing, send_a, recv_a)
+    stats = exchange("shard", n, lambda peer: stat_ref, stat_in, send_b, recv_b)
+    landing[me] = gram_ref[me]
+    stat_in[me] = stat_ref[...]
+    for copy in first:
+        copy.wait()
+    value = add_up(landing, n)
+    done[...] = value
+    full[me] = value
+    second = exchange("shard", n, lambda peer: done, full, send_c, recv_c)
+    for copy in stats:
+        copy.wait()
+    value = add_up(stat_in, n)
+    stat_sum[...] = value
+    seg_in[seg] = value
+    third = exchange("segment", segments, lambda peer: stat_sum, seg_in, send_d, recv_d)
+    pieces = factor_pieces(slots, full, work, side, inv_ref)
+    hops = n // 2
+
+    def between(hop):
+        if hop == 0:
+            for copy in second:
+                copy.wait()
+        for i, piece in enumerate(pieces):
+            if i * hops // len(pieces) == hop:
+                piece()
+
+    own = ring_scatter(n, slots, part_ref, sums, got, send_e, recv_e, between)
     mine[...] = jnp.zeros_like(mine)
     for slot in range(slots):
-        value = mm(own_ref[slot], inv_ref[slot], (1, 1))
-        full_ref[slot, me] = value.astype(BF16)
+        value = mm(own[slot], inv_ref[slot], (1, 1))
+        basis_ref[slot, me] = value.astype(BF16)
         mine[slot : slot + 1] = jnp.sum(value * value, axis=0, keepdims=True)
         right_ref[slot] = value
-    copies = exchange("shard", n, lambda peer: mine, sq_in, send_a, recv_a)
+    squares = exchange("shard", n, lambda peer: mine, sq_in, send_f, recv_f)
     sq_in[me] = mine[...]
-    ring_gather(n, slots, full_ref, send_b, recv_b)
-    for copy in copies:
+    ring_gather(n, slots, basis_ref, send_g, recv_g)
+    for copy in squares + third:
         copy.wait()
-    total = sq_in[0]
-    for i in range(1, n):
-        total = total + sq_in[i]
-    scale = math.sqrt(cols) * lax.rsqrt(total + 1.0)
+    total_ref[...] = add_up(seg_in, segments)
+    scale = math.sqrt(cols) * lax.rsqrt(add_up(sq_in, n) + 1.0)
     for slot in range(slots):
         right_ref[slot] = right_ref[slot] * scale[slot : slot + 1]
 
@@ -291,9 +333,10 @@
 
     @pl.when(keep)
     def _():
-        ortho = mm(proj_ref[0], inv_ref[0], (1, 1))
-        half = ortho.astype(BF16)
-        fix = lax.dot_general(half, basis_ref[0], (((1,), (1,)), ((), ())), preferred_element_type=F32)
+        high, low = split(proj_ref[0])
+        top, rest = split(inv_ref[0])
+        ortho = dot(high, top, (1, 1)) + (dot(high, rest, (1, 1)) + dot(low, top, (1, 1)))
+        fix = dot(ortho.astype(BF16), basis_ref[0], (1, 1))
         moment_ref[0] = (block_ref[0].astype(F32) - (1.0 - MOMENTUM) * fix).astype(BF16)
         left_ref[0] = (scale_ref[0] * ortho).astype(BF16)
 
@@ -334,7 +377,8 @@
         name="gather_basis",
     )(right_basis).reshape(slots, cols, rank)
 
-    tile = math.gcd(rows_dev, 256)
+    half = rank // 2
+    tile = math.gcd(rows_dev, 768)
     tiles = rows_dev // tile
     per_tile = pl.BlockSpec((1, tile, cols), lambda s, i: (s, i, 0))
     proj_tile = pl.BlockSpec((1, tile, rank), lambda s, i: (s, i, 0))
@@ -347,12 +391,18 @@
         grid=(slots, tiles),
         out_shape=(
             shape((slots, rows_dev, rank), F32),
-            shape((slots, rank, rank), F32),
+            shape((slots, 3, half, half), F32),
             shape((slots, cols, rank), F32),
             shape((slots, 8, cols), F32),
         ),
         in_specs=[per_tile, per_slot(cols, rank)],
-        out_specs=(proj_tile, per_slot(rank, rank), per_slot(cols, rank), per_slot(8, cols)),
+        out_specs=(
+            proj_tile,
+            pl.BlockSpec((1, 3, half, half), lambda s, i: (s, 0, 0, 0)),
+            per_slot(cols, rank),
+            per_slot(8, cols),
+        ),
+        scratch_shapes=[pltpu.VMEM((2, rank, rank), F32)],
         compiler_params=pltpu.CompilerParams(vmem_limit_bytes=VMEM_LIMIT),
         name="project",
     )(buffer, basis)
@@ -362,55 +412,40 @@
     local_elems = count.astype(F32) * float(rows_dev * cols)
     odd = lax.broadcasted_iota(jnp.int32, (8, 128), 0) % 2 == 1
     stat = jnp.where(odd, local_elems, local_sq)
-    chunk = slots * rank // n
-
-    full_gram, total, own = pl.pallas_call(
-        functools.partial(reduce_kernel, n, segments, slots),
+    chunk = slots * 3 * half // n
+
+    total, inverse, right, half_right = pl.pallas_call(
+        functools.partial(reduce_kernel, n, segments, slots, cols),
         out_shape=(
-            shape((n, chunk, rank), F32),
             shape((8, 128), F32),
+            shape((slots, rank, rank), F32),
             shape((slots, width, rank), F32),
+            shape((slots, n, width, rank), BF16),
         ),
         in_specs=[vmem()] * 3,
-        out_specs=(vmem(),) * 3,
+        out_specs=(vmem(),) * 4,
         scratch_shapes=[
-            pltpu.VMEM((n, chunk, rank), F32),
-            pltpu.VMEM((chunk, rank), F32),
+            pltpu.VMEM((n, chunk, half), F32),
+            pltpu.VMEM((n, chunk, half), F32),
+            pltpu.VMEM((chunk, half), F32),
             pltpu.VMEM((n, 8, 128), F32),
             pltpu.VMEM((8, 128), F32),
             pltpu.VMEM((segments, 8, 128), F32),
             pltpu.VMEM((slots, 2, hops, width, rank), LINK),
             pltpu.VMEM((slots, 2, hops, width, rank), LINK),
+            pltpu.VMEM((slots, half, half), F32),
+            pltpu.VMEM((slots, half, half), F32),
+            pltpu.VMEM((8, rank), F32),
+            pltpu.VMEM((n, 8, rank), F32),
             dma((n,)), dma((n,)), dma((n,)), dma((n,)), dma((n,)), dma((n,)),
             dma((segments,)), dma((segments,)),
+            dma((slots, 2, hops)), dma((slots, 2, hops)),
+            dma((n,)), dma((n,)),
             dma((slots, 2, hops)), dma((slots, 2, hops)),
         ],
         compiler_params=comm(1),
         name="reduce",
-    )(gram.reshape(n, chunk, rank), stat, part.reshape(slots, n, width, rank))
-
-    inverse = pl.pallas_call(
-        functools.partial(factor_kernel, slots),
-        out_shape=shape((slots, rank, rank), F32),
-        in_specs=[vmem()],
-        out_specs=vmem(),
-        name="factor",
-    )(full_gram.reshape(slots, rank, rank))
-
-    right, half_right = pl.pallas_call(
-        functools.partial(right_kernel, n, slots, cols),
-        out_shape=(shape((slots, width, rank), F32), shape((slots, n, width, rank), BF16)),
-        in_specs=[vmem()] * 2,
-        out_specs=(vmem(),) * 2,
-        scratch_shapes=[
-            pltpu.VMEM((8, rank), F32),
-            pltpu.VMEM((n, 8, rank), F32),
-            dma((n,)), dma((n,)),
-            dma((slots, 2, hops)), dma((slots, 2, hops)),
-        ],
-        compiler_params=comm(2),
-        name="right",
-    )(own, inverse)
+    )(gram.reshape(n, chunk, half), stat, part.reshape(slots, n, width, rank))
 
     clip = jnp.minimum(1.0, CLIP_RMS * lax.rsqrt(jnp.maximum(total[0, 0] / total[1, 0], SQUARE_FLOOR)))
     scale = (clip * math.sqrt(rows_all)).reshape(1)

time: 261 us -> 194 us (0.74)
  Pallas kernels: 249 us -> 184 us
    pallas_call x3 -> x1, Pallas kernels: 151 us -> 101 us  [body(): pl.pallas_call(functools.partial(reduce_kernel, n, segments, slots, cols)...]
    pallas_call x1, Pallas kernels: 40 us -> 31 us  [body(): pl.pallas_call(project_kernel, grid=(slots, tiles), out_shape=(shape((slo...]
    pallas_call x1, Pallas kernels: 26.5 us -> 20.3 us  [body(): pl.pallas_call(final_kernel, grid=(slots, tiles), out_shape=(shape(buffer...]
where the time goes in v2:
time: 194 us; the launch traced here: 193 us
  Pallas kernels  184 us (95%)
  other arithmetic  4.81 us (2%)
  between operations  2.7 us (1%)
    pallas_call x1, Pallas kernels, body(): pl.pallas_call(functools.partial(reduce_kernel, n, segments, slots, cols)...  101 us
    pallas_call x1, Pallas kernels, body(): pl.pallas_call(functools.partial(gather_kernel, n, slots), out_shape=shap...  31.5 us
    pallas_call x1, Pallas kernels, body(): pl.pallas_call(project_kernel, grid=(slots, tiles), out_shape=(shape((slo...  31 us
    pallas_call x1, Pallas kernels, body(): pl.pallas_call(final_kernel, grid=(slots, tiles), out_shape=(shape(buffer...  20.3 us

profile of v2, /device:TPU:0, one launch (start us, length us, event | category | flops | bytes accessed | tf_op | source)
XLA Modules:
  0.0 192.8 jit_solution(3797985886869750300)
XLA Ops:
  1.3 31.5 %gather_basis.1 = bf16[2,8,288,256]{3,2,1,0:T(8,128)(2,1)} custom-call(bf16[2,288,256]{2,1,0:T(8,128)(2,1)} %basis_ref.1), custom_call_target="tpu_custom_call" | custom-call | tf_op jit(solution)/shard_map/gather_basis/pallas_call | solution.py:370
  32.8 31.0 %project.1 = (f32[2,2304,256]{2,1,0:T(8,128)}, f32[2,3,128,128]{3,2,1,0:T(8,128)}, f32[2,2304,256]{2,1,0:T(8,128)}, f32[2,8,2304]{2,1,0:T(8,128)}) custom-call(bf16[2,2304,2304]{2,1,0:T(8,128)(2,1)} %block_ref.3, bf16[2,2304,256]{2,1,0:T(8,128)(2,1)} %bitcast.9), custom_call_target="tpu_custom_call" | custom-call | tf_op jit(solution)/shard_map/project/pallas_call | solution.py:389
  63.8 1.0 reduce_sum.18
  64.8 0.6 select_reduce_fusion
  65.4 1.2 fusion.stat_ref
  66.6 101.3 %reduce.1 = (f32[8,128]{1,0:T(8,128)}, f32[2,256,256]{2,1,0:T(8,128)}, f32[2,288,256]{2,1,0:T(8,128)}, bf16[2,8,288,256]{3,2,1,0:T(8,128)(2,1)}) custom-call(f32[8,96,128]{2,1,0:T(8,128)} %bitcast.12, f32[8,128]{1,0:T(8,128)} %fusion.stat_ref, f32[2,8,288,256]{3,2,1,0:T(8,128)} %bitcast.10), custom_call_target="tpu_custom_call" | custom-call | tf_op jit(solution)/shard_map/reduce/pallas_call | solution.py:417
  167.9 1.3 fusion.1
  170.5 2.0 %broadcast_select_fusion = f32[2,288,256]{2,1,0:T(8,128)} fusion(f32[2,288,256]{2,1,0:T(8,128)} %get-tuple-element.22, pred[2]{0:T(512)(128)(4,1)S(1)} %iota_compare_fusion), kind=kLoop, calls=%fused_computation | loop fusion | flops 147456 | bytes 1179650 | tf_op jit(solution)/shard_map/jit(_where)/select_n | solution.py:462
  172.5 20.3 %final.1 = (bf16[2,2304,2304]{2,1,0:T(8,128)(2,1)}, bf16[2,2304,256]{2,1,0:T(8,128)(2,1)}) custom-call(f32[1]{0:T(128)} %bitcast.4.scale_ref, s32[1]{0:T(128)} %copy.6.count_ref, bf16[2,2304,2304]{2,1,0:T(8,128)(2,1)} %block_ref.3, f32[2,2304,256]{2,1,0:T(8,128)} %get-tuple-element.17.proj_ref, f32[2,256,256]{2,1,0:T(8,128)} %get-tuple-element.18.inv_ref, ...), custom_call_target="tpu_custom_call" | custom-call | tf_op jit(solution)/shard_map/final/pallas_call | solution.py:453
  (3 shorter events, 0.0 us)
